TPU v7x, 32 devices: a whole 2x2x4 slice. The times are simulated.
32 devices in a mesh: wide: 8 (over z, x), narrow: 4 (over y, core).
Axes of the slice: x: 2, y: 2, z: 4, core: 2. Of those that a mesh axis runs over, the one named last changes fastest.
Arguments:
- cost: float32 [1024, 16384], P('wide', 'narrow'), may hold values from 0 to 2
- plan: float32 [1024, 16384], P('wide', 'narrow'), may hold values from 0 to 2
- row_mass: float32 [1024], P('wide'), may hold values from 4096 to 28672
- col_mass: float32 [16384], P('narrow'), may hold values from 256 to 1792
- row_dual: float32 [1024], P('wide'), may hold values from -3 to 3
- col_dual: float32 [16384], P('narrow'), may hold values from -3 to 3
Outputs:
- plan_out: float32 [1024, 16384], P('wide', 'narrow')
- row_out: float32 [1024], P('wide')
- col_out: float32 [16384], P('narrow')
All inputs are finite; a program needn't handle non-finite values.
Results may differ from a plain program's by a relative error of at most 0.0001.
Values sent between devices are 32-bit elements; how exact they have to be, the bound alone decides.
A program may use at most 64 MiB of HBM per device.

v0:
```python
import math
import jax
import jax.numpy as jnp
from jax import lax
from jax.sharding import PartitionSpec as P

ITERS = 4


def shards(cost, plan, row_mass, col_mass, row_dual, col_dual):
    wide_count = lax.axis_size("wide")
    narrow_count = lax.axis_size("narrow")
    total_rows = plan.shape[0] * wide_count
    total_cols = plan.shape[1] * narrow_count
    step_base = 0.9 / math.sqrt(total_rows + total_cols)
    weight = jnp.float32(step_base)
    for step in range(ITERS):
        primal_step = step_base / weight
        dual_step = step_base * weight
        fresh = jnp.maximum(
            plan - primal_step * (cost - row_dual[:, None] - col_dual[None, :]), 0.0
        )
        change = fresh - plan
        extrap = fresh + change
        moved = jnp.sum(change * change)
        row_total = lax.psum(jnp.sum(extrap, axis=1), "narrow")
        new_row = row_dual + dual_step * (row_mass - row_total)
        row_square = jnp.sum((new_row - row_dual) ** 2)
        col_local = jnp.sum(extrap, axis=0)
        col_total = lax.psum(col_local, "wide")
        new_col = col_dual + dual_step * (col_mass - col_total)
        col_share = jnp.sum((new_col - col_dual) ** 2) / wide_count
        dual_share = row_square / narrow_count + col_share
        moved_all = lax.psum(moved, ("wide", "narrow"))
        dual_moved = lax.psum(dual_share, ("wide", "narrow"))
        weight = jnp.sqrt(weight * jnp.sqrt((dual_moved + 1.0) / (moved_all + 1.0)))
        plan, row_dual, col_dual = (fresh, new_row, new_col)
    return (plan, row_dual, col_dual)


def solution(mesh):
    in_specs = (
        P("wide", "narrow"),
        P("wide", "narrow"),
        P("wide"),
        P("narrow"),
        P("wide"),
        P("narrow"),
    )
    out_specs = (P("wide", "narrow"), P("wide"), P("narrow"))
    return jax.shard_map(shards, mesh=mesh, in_specs=in_specs, out_specs=out_specs, check_vma=False)
```

profile of v0, /device:TPU:0, one launch (start us, length us, event | category | flops | bytes accessed | tf_op | source)
XLA Modules:
  0.0 314.4 jit_solution(7714371782723744070)
XLA Ops:
  0.6 0.0 copy-start.1
  0.6 0.0 copy-start.3
  0.7 0.0 copy-start.2
  0.7 0.0 copy-start.4
  0.7 0.0 copy-start
  0.7 4.2 %multiply_reduce_fusion.2 = (f32[]{:T(128)}, f32[4096]{0:T(1024)S(1)}, f32[128]{0:T(128)S(1)}) fusion(f32[128,4096]{1,0:T(8,128)} %param.7, f32[4096]{0:T(1024)} %param.11, f32[128,4096]{1,0:T(8,128)} %param.6, f32[128]{0:T(128)} %param.10), kind=kLoop, calls=%fused_computation.6 | loop fusion | flops 5238655 | bytes 4228100 | tf_op jit(solution)/shard_map/reduce_sum | solution.py:25
  4.9 38.8 %psum.99 = f32[4096]{0:T(1024)S(1)} all-reduce(f32[4096]{0:T(1024)S(1)} %get-tuple-element.12), channel_id=1, replica_groups=mesh['wide'=8,'narrow'=4] {'wide'}, use_global_device_ids=true, to_apply=%region_4.0 | all-reduce | flops 4096 | bytes 32768 | tf_op jit(solution)/shard_map/psum | solution.py:30
  43.7 5.6 %psum.98 = f32[128]{0:T(128)S(1)} all-reduce(f32[128]{0:T(128)S(1)} %get-tuple-element.13), channel_id=1, replica_groups=mesh['wide'=8,'narrow'=4] {'narrow'}, use_global_device_ids=true, to_apply=%region_1.0 | all-reduce | flops 128 | bytes 1024 | tf_op jit(solution)/shard_map/psum | solution.py:26
  49.3 0.0 copy-done.3
  49.3 0.0 copy-done.4
  49.3 0.6 multiply_reduce_fusion.8
  50.6 0.0 copy-done.1
  50.6 0.0 copy-done.2
  50.6 0.6 multiply_reduce_fusion.5
  51.9 37.2 %all-reduce.2 = (f32[]{:T(128)}, f32[]{:T(128)}) all-reduce(f32[]{:T(128)S(6)} %add.94, f32[]{:T(128)} %get-tuple-element.11), channel_id=1, replica_groups=mesh['wide'=8,'narrow'=4] {'wide','narrow'}, use_global_device_ids=true, to_apply=%region_6.0 | all-reduce | flops 2 | bytes 16 | tf_op jit(solution)/shard_map/psum | solution.py:35
  90.5 0.0 copy-done
  90.5 3.7 %multiply_reduce_fusion.1 = (f32[]{:T(128)}, f32[128]{0:T(128)S(1)}, f32[4096]{0:T(1024)S(1)}) fusion(f32[4096]{0:T(1024)S(1)} %get-tuple-element.30, f32[128,4096]{1,0:T(8,128)} %param.6, f32[128]{0:T(128)S(1)} %get-tuple-element.32, f32[]{:T(128)S(6)} %div.39, f32[128,4096]{1,0:T(8,128)S(1)} %copy-done, f32[4096]{0:T(1024)S(1)} %copy-done.1, ...), kind=kLoop, calls=%fused_computation.4 | loop fusion | flops 7860095 | bytes 4245000 | tf_op jit(solution)/shard_map/reduce_sum | solution.py:25
  94.2 6.9 %psum.102 = f32[128]{0:T(128)S(1)} all-reduce(f32[128]{0:T(128)S(1)} %get-tuple-element.9), channel_id=1, replica_groups=mesh['wide'=8,'narrow'=4] {'narrow'}, use_global_device_ids=true, to_apply=%region_10.0 | all-reduce | flops 128 | bytes 1024 | tf_op jit(solution)/shard_map/psum | solution.py:26
  101.1 0.6 multiply_reduce_fusion.7
  102.4 35.6 %psum.103 = f32[4096]{0:T(1024)S(1)} all-reduce(f32[4096]{0:T(1024)S(1)} %get-tuple-element.10), channel_id=1, replica_groups=mesh['wide'=8,'narrow'=4] {'wide'}, use_global_device_ids=true, to_apply=%region_13.0 | all-reduce | flops 4096 | bytes 32768 | tf_op jit(solution)/shard_map/psum | solution.py:30
  138.0 0.6 multiply_reduce_fusion.4
  139.2 37.1 %all-reduce.1 = (f32[]{:T(128)}, f32[]{:T(128)}) all-reduce(f32[]{:T(128)S(6)} %add.100, f32[]{:T(128)} %get-tuple-element.8), channel_id=1, replica_groups=mesh['wide'=8,'narrow'=4] {'wide','narrow'}, use_global_device_ids=true, to_apply=%region_15.0 | all-reduce | flops 2 | bytes 16 | tf_op jit(solution)/shard_map/psum | solution.py:35
  177.8 4.2 %multiply_reduce_fusion = (f32[]{:T(128)}, f32[128]{0:T(128)S(1)}, f32[4096]{0:T(1024)S(1)}) fusion(f32[4096]{0:T(1024)S(1)} %get-tuple-element.26, f32[128,4096]{1,0:T(8,128)} %param.6, f32[128]{0:T(128)S(1)} %get-tuple-element.28, f32[]{:T(128)S(6)} %div.43, f32[4096]{0:T(1024)S(1)} %get-tuple-element.30, f32[128]{0:T(128)S(1)} %get-tuple-element.32, ...), kind=kLoop, calls=%fused_computation.2 | loop fusion | flops 10481535 | bytes 4261900 | tf_op jit(solution)/shard_map/reduce_sum | solution.py:25
  182.0 7.2 %psum.106 = f32[128]{0:T(128)S(1)} all-reduce(f32[128]{0:T(128)S(1)} %get-tuple-element.6), channel_id=1, replica_groups=mesh['wide'=8,'narrow'=4] {'narrow'}, use_global_device_ids=true, to_apply=%region_19.0 | all-reduce | flops 128 | bytes 1024 | tf_op jit(solution)/shard_map/psum | solution.py:26
  189.2 0.6 multiply_reduce_fusion.6
  190.5 35.3 %psum.107 = f32[4096]{0:T(1024)S(1)} all-reduce(f32[4096]{0:T(1024)S(1)} %get-tuple-element.7), channel_id=1, replica_groups=mesh['wide'=8,'narrow'=4] {'wide'}, use_global_device_ids=true, to_apply=%region_22.0 | all-reduce | flops 4096 | bytes 32768 | tf_op jit(solution)/shard_map/psum | solution.py:30
  225.8 0.6 multiply_reduce_fusion.3
  227.0 37.3 %all-reduce = (f32[]{:T(128)}, f32[]{:T(128)}) all-reduce(f32[]{:T(128)S(6)} %add.106, f32[]{:T(128)} %get-tuple-element.5), channel_id=1, replica_groups=mesh['wide'=8,'narrow'=4] {'wide','narrow'}, use_global_device_ids=true, to_apply=%region_24.0 | all-reduce | flops 2 | bytes 16 | tf_op jit(solution)/shard_map/psum | solution.py:35
  265.8 4.9 %fusion.6 = (f32[4096]{0:T(1024)S(1)}, f32[128]{0:T(128)S(1)}, f32[128,4096]{1,0:T(8,128)}) fusion(f32[4096]{0:T(1024)S(1)} %get-tuple-element.26, f32[128,4096]{1,0:T(8,128)} %param.6, f32[128]{0:T(128)S(1)} %get-tuple-element.28, f32[]{:T(128)S(6)} %div.43, f32[4096]{0:T(1024)S(1)} %get-tuple-element.30, f32[128]{0:T(128)S(1)} %get-tuple-element.32, ...), kind=kLoop, calls=%fused_computation.17 | loop fusion | flops 12054400 | bytes 6375948 | tf_op jit(solution)/shard_map/reduce_sum | solution.py:29
  270.7 36.8 %psum.111 = f32[4096]{0:T(1024)S(1)} all-reduce(f32[4096]{0:T(1024)S(1)} %get-tuple-element.3), channel_id=1, replica_groups=mesh['wide'=8,'narrow'=4] {'wide'}, use_global_device_ids=true, to_apply=%region_30.0 | all-reduce | flops 4096 | bytes 32768 | tf_op jit(solution)/shard_map/psum | solution.py:30
  307.5 0.6 multiply_add_fusion
  308.1 5.7 %psum.110 = f32[128]{0:T(128)S(1)} all-reduce(f32[128]{0:T(128)S(1)} %get-tuple-element.4), channel_id=1, replica_groups=mesh['wide'=8,'narrow'=4] {'narrow'}, use_global_device_ids=true, to_apply=%region_28.0 | all-reduce | flops 128 | bytes 1024 | tf_op jit(solution)/shard_map/psum | solution.py:26
  313.9 0.5 multiply_add_fusion.4
Async XLA Ops:
  0.6 49.9 %copy-start.1 = (f32[4096]{0:T(1024)S(1)}, f32[4096]{0:T(1024)}, u32[]{:S(2)}) copy-start(f32[4096]{0:T(1024)} %param.11) | copy-start | bytes 49156
  0.6 48.7 %copy-start.3 = (f32[128]{0:T(128)S(1)}, f32[128]{0:T(128)}, u32[]{:S(2)}) copy-start(f32[128]{0:T(128)} %param.10) | copy-start | bytes 1540
  0.7 49.9 %copy-start.2 = (f32[4096]{0:T(1024)S(1)}, f32[4096]{0:T(1024)}, u32[]{:S(2)}) copy-start(f32[4096]{0:T(1024)} %param.9) | copy-start | bytes 49156
  0.7 48.7 %copy-start.4 = (f32[128]{0:T(128)S(1)}, f32[128]{0:T(128)}, u32[]{:S(2)}) copy-start(f32[128]{0:T(128)} %param.8) | copy-start | bytes 1540
  0.7 89.8 %copy-start = (f32[128,4096]{1,0:T(8,128)S(1)}, f32[128,4096]{1,0:T(8,128)}, u32[]{:S(2)}) copy-start(f32[128,4096]{1,0:T(8,128)} %param.7) | copy-start | bytes 6291460
where the time goes:
time: 315 us; the launch traced here: 314 us
  blocking collectives  284 us (90%)
  other arithmetic  21.7 us (7%)
  between operations  9.03 us (3%)
    psum x4, blocking collectives, shards(): col_total = lax.psum(col_local, 'wide')  147 us
    psum x3, blocking collectives, shards(): dual_moved = lax.psum(dual_share, ('wide', 'narrow'))  112 us
    psum x4, blocking collectives, shards(): row_total = lax.psum(jnp.sum(extrap, axis=1), 'narrow')  25.5 us
    reduce_sum x3, other arithmetic, shards(): moved = jnp.sum(change * change)  12.1 us

commit v1 on v0

--- a/solution.py
+++ b/solution.py
@@ -27,7 +27,12 @@
         new_row = row_dual + dual_step * (row_mass - row_total)
         row_square = jnp.sum((new_row - row_dual) ** 2)
         col_local = jnp.sum(extrap, axis=0)
-        col_total = lax.psum(col_local, "wide")
+
+        def carry_matrix(v0):
+            y1 = jnp.sum(jax.lax.all_gather(v0, "wide"), 0)
+            return y1
+
+        col_total = carry_matrix(col_local)
         new_col = col_dual + dual_step * (col_mass - col_total)
         col_share = jnp.sum((new_col - col_dual) ** 2) / wide_count
         dual_share = row_square / narrow_count + col_share

time: 315 us -> 297 us (0.943)
  blocking collectives: 284 us -> 265 us
    psum x4 -> x0, blocking collectives: 147 us -> none  [shards(): col_total = lax.psum(col_local, 'wide')]
    all_gather x0 -> x4, blocking collectives: none -> 122 us  [carry_matrix(): y1 = jnp.sum(jax.lax.all_gather(v0, 'wide'), 0)]
    psum x3, blocking collectives: 112 us -> 116 us  [shards(): dual_moved = lax.psum(dual_share, ('wide', 'narrow'))]
where the time goes in v1:
time: 297 us; the launch traced here: 296 us
  blocking collectives  265 us (89%)
  other arithmetic  21.9 us (7%)
  between operations  9.07 us (3%)
    all_gather x4, blocking collectives, carry_matrix(): y1 = jnp.sum(jax.lax.all_gather(v0, 'wide'), 0)  122 us
    psum x3, blocking collectives, shards(): dual_moved = lax.psum(dual_share, ('wide', 'narrow'))  116 us
    psum x4, blocking collectives, shards(): row_total = lax.psum(jnp.sum(extrap, axis=1), 'narrow')  27.1 us
    reduce_sum x3, other arithmetic, shards(): moved = jnp.sum(change * change)  12.1 us

profile of v1, /device:TPU:0, one launch (start us, length us, event | category | flops | bytes accessed | tf_op | source)
XLA Modules:
  0.0 296.3 jit_solution(10320594225707737295)
XLA Ops:
  0.6 0.0 copy-start.1
  0.6 0.0 copy-start.3
  0.7 0.0 copy-start.2
  0.7 0.0 copy-start.4
  0.7 0.0 copy-start
  0.7 4.2 %multiply_reduce_fusion.2 = (f32[]{:T(128)}, f32[4096]{0:T(1024)S(1)}, f32[128]{0:T(128)S(1)}) fusion(f32[128,4096]{1,0:T(8,128)} %param.7, f32[4096]{0:T(1024)} %param.11, f32[128,4096]{1,0:T(8,128)} %param.6, f32[128]{0:T(128)} %param.10), kind=kLoop, calls=%fused_computation.6 | loop fusion | flops 5238655 | bytes 4228100 | tf_op jit(solution)/shard_map/reduce_sum | solution.py:25
  4.9 8.4 %psum.70 = f32[128]{0:T(128)S(1)} all-reduce(f32[128]{0:T(128)S(1)} %get-tuple-element.13), channel_id=1, replica_groups=mesh['wide'=8,'narrow'=4] {'narrow'}, use_global_device_ids=true, to_apply=%region_1.0 | all-reduce | flops 128 | bytes 1024 | tf_op jit(solution)/shard_map/psum | solution.py:26
  13.2 0.0 copy-done.3
  13.2 0.0 copy-done.4
  13.2 0.6 multiply_reduce_fusion.8
  14.5 30.9 %all-gather = f32[32768]{0:T(1024)S(1)} all-gather(f32[4096]{0:T(1024)S(1)} %get-tuple-element.12), channel_id=2, replica_groups=mesh['wide'=8,'narrow'=4] {'wide'}, dimensions={0}, use_global_device_ids=true | all-gather | bytes 147456 | tf_op jit(solution)/shard_map/all_gather | solution.py:32
  45.4 0.0 copy-done.1
  45.4 0.0 copy-done.2
  45.4 0.6 multiply_reduce_fusion.5
  46.7 38.8 %all-reduce.2 = (f32[]{:T(128)}, f32[]{:T(128)}) all-reduce(f32[]{:T(128)S(6)} %add.86, f32[]{:T(128)} %get-tuple-element.11), channel_id=1, replica_groups=mesh['wide'=8,'narrow'=4] {'wide','narrow'}, use_global_device_ids=true, to_apply=%region_6.0 | all-reduce | flops 2 | bytes 16 | tf_op jit(solution)/shard_map/psum | solution.py:40
  86.9 0.0 copy-done
  87.0 3.7 %multiply_reduce_fusion.1 = (f32[]{:T(128)}, f32[128]{0:T(128)S(1)}, f32[4096]{0:T(1024)S(1)}) fusion(f32[4096]{0:T(1024)S(1)} %get-tuple-element.30, f32[128,4096]{1,0:T(8,128)} %param.6, f32[128]{0:T(128)S(1)} %get-tuple-element.32, f32[]{:T(128)S(6)} %div.39, f32[128,4096]{1,0:T(8,128)S(1)} %copy-done, f32[4096]{0:T(1024)S(1)} %copy-done.1, ...), kind=kLoop, calls=%fused_computation.4 | loop fusion | flops 7860095 | bytes 4245000 | tf_op jit(solution)/shard_map/reduce_sum | solution.py:25
  90.7 6.8 %psum.73 = f32[128]{0:T(128)S(1)} all-reduce(f32[128]{0:T(128)S(1)} %get-tuple-element.9), channel_id=1, replica_groups=mesh['wide'=8,'narrow'=4] {'narrow'}, use_global_device_ids=true, to_apply=%region_10.0 | all-reduce | flops 128 | bytes 1024 | tf_op jit(solution)/shard_map/psum | solution.py:26
  97.5 0.6 multiply_reduce_fusion.7
  98.7 30.6 %all-gather.1 = f32[32768]{0:T(1024)S(1)} all-gather(f32[4096]{0:T(1024)S(1)} %get-tuple-element.10), channel_id=3, replica_groups=mesh['wide'=8,'narrow'=4] {'wide'}, dimensions={0}, use_global_device_ids=true | all-gather | bytes 147456 | tf_op jit(solution)/shard_map/all_gather | solution.py:32
  129.4 0.6 multiply_reduce_fusion.4
  130.6 38.1 %all-reduce.1 = (f32[]{:T(128)}, f32[]{:T(128)}) all-reduce(f32[]{:T(128)S(6)} %add.92, f32[]{:T(128)} %get-tuple-element.8), channel_id=1, replica_groups=mesh['wide'=8,'narrow'=4] {'wide','narrow'}, use_global_device_ids=true, to_apply=%region_15.0 | all-reduce | flops 2 | bytes 16 | tf_op jit(solution)/shard_map/psum | solution.py:40
  170.1 4.2 %multiply_reduce_fusion = (f32[]{:T(128)}, f32[128]{0:T(128)S(1)}, f32[4096]{0:T(1024)S(1)}) fusion(f32[4096]{0:T(1024)S(1)} %get-tuple-element.26, f32[128,4096]{1,0:T(8,128)} %param.6, f32[128]{0:T(128)S(1)} %get-tuple-element.28, f32[]{:T(128)S(6)} %div.43, f32[4096]{0:T(1024)S(1)} %get-tuple-element.30, f32[128]{0:T(128)S(1)} %get-tuple-element.32, ...), kind=kLoop, calls=%fused_computation.2 | loop fusion | flops 10481535 | bytes 4261900 | tf_op jit(solution)/shard_map/reduce_sum | solution.py:25
  174.3 6.0 %psum.76 = f32[128]{0:T(128)S(1)} all-reduce(f32[128]{0:T(128)S(1)} %get-tuple-element.6), channel_id=1, replica_groups=mesh['wide'=8,'narrow'=4] {'narrow'}, use_global_device_ids=true, to_apply=%region_19.0 | all-reduce | flops 128 | bytes 1024 | tf_op jit(solution)/shard_map/psum | solution.py:26
  180.3 0.6 multiply_reduce_fusion.6
  181.6 30.5 %all-gather.2 = f32[32768]{0:T(1024)S(1)} all-gather(f32[4096]{0:T(1024)S(1)} %get-tuple-element.7), channel_id=4, replica_groups=mesh['wide'=8,'narrow'=4] {'wide'}, dimensions={0}, use_global_device_ids=true | all-gather | bytes 147456 | tf_op jit(solution)/shard_map/all_gather | solution.py:32
  212.2 0.6 multiply_reduce_fusion.3
  213.4 38.7 %all-reduce = (f32[]{:T(128)}, f32[]{:T(128)}) all-reduce(f32[]{:T(128)S(6)} %add.98, f32[]{:T(128)} %get-tuple-element.5), channel_id=1, replica_groups=mesh['wide'=8,'narrow'=4] {'wide','narrow'}, use_global_device_ids=true, to_apply=%region_24.0 | all-reduce | flops 2 | bytes 16 | tf_op jit(solution)/shard_map/psum | solution.py:40
  253.7 4.9 %fusion.6 = (f32[4096]{0:T(1024)S(1)}, f32[128]{0:T(128)S(1)}, f32[128,4096]{1,0:T(8,128)}) fusion(f32[4096]{0:T(1024)S(1)} %get-tuple-element.26, f32[128,4096]{1,0:T(8,128)} %param.6, f32[128]{0:T(128)S(1)} %get-tuple-element.28, f32[]{:T(128)S(6)} %div.43, f32[4096]{0:T(1024)S(1)} %get-tuple-element.30, f32[128]{0:T(128)S(1)} %get-tuple-element.32, ...), kind=kLoop, calls=%fused_computation.17 | loop fusion | flops 12054400 | bytes 6375948 | tf_op jit(solution)/shard_map/reduce_sum | solution.py:29
  258.6 6.0 %psum.79 = f32[128]{0:T(128)S(1)} all-reduce(f32[128]{0:T(128)S(1)} %get-tuple-element.4), channel_id=1, replica_groups=mesh['wide'=8,'narrow'=4] {'narrow'}, use_global_device_ids=true, to_apply=%region_28.0 | all-reduce | flops 128 | bytes 1024 | tf_op jit(solution)/shard_map/psum | solution.py:26
  264.5 0.5 multiply_add_fusion.4
  265.1 30.5 %all-gather.3 = f32[32768]{0:T(1024)S(1)} all-gather(f32[4096]{0:T(1024)S(1)} %get-tuple-element.3), channel_id=5, replica_groups=mesh['wide'=8,'narrow'=4] {'wide'}, dimensions={0}, use_global_device_ids=true | all-gather | bytes 147456 | tf_op jit(solution)/shard_map/all_gather | solution.py:32
  295.6 0.6 multiply_add_fusion
  (8 shorter events, 0.3 us)
Async XLA Ops:
  0.6 44.8 %copy-start.1 = (f32[4096]{0:T(1024)S(1)}, f32[4096]{0:T(1024)}, u32[]{:S(2)}) copy-start(f32[4096]{0:T(1024)} %param.11) | copy-start | bytes 49156
  0.6 12.6 %copy-start.3 = (f32[128]{0:T(128)S(1)}, f32[128]{0:T(128)}, u32[]{:S(2)}) copy-start(f32[128]{0:T(128)} %param.10) | copy-start | bytes 1540
  0.7 44.8 %copy-start.2 = (f32[4096]{0:T(1024)S(1)}, f32[4096]{0:T(1024)}, u32[]{:S(2)}) copy-start(f32[4096]{0:T(1024)} %param.9) | copy-start | bytes 49156
  0.7 12.6 %copy-start.4 = (f32[128]{0:T(128)S(1)}, f32[128]{0:T(128)}, u32[]{:S(2)}) copy-start(f32[128]{0:T(128)} %param.8) | copy-start | bytes 1540
  0.7 86.3 %copy-start = (f32[128,4096]{1,0:T(8,128)S(1)}, f32[128,4096]{1,0:T(8,128)}, u32[]{:S(2)}) copy-start(f32[128,4096]{1,0:T(8,128)} %param.7) | copy-start | bytes 6291460
